TPU v7x, 512 devices: a whole 4x8x8 slice. The times are simulated.
512 devices in a mesh: row: 32 (over z, x), col: 16 (over y, core).
Axes of the slice: x: 4, y: 8, z: 8, core: 2. Of those that a mesh axis runs over, the one named last changes fastest.
Arguments:
- lower: bfloat16 [32, 3, 512, 2, 512], P('row', None, None, None, 'col'), as said below
- rhs: bfloat16 [32, 3, 512, 8192], P('row', None, None, 'col'), may hold values from -6 to 6
- tile_map: int32 [16], replicated, may hold values from 0 to 15, each once
Outputs:
- overwritten: bfloat16 [32, 3, 512, 8192], P('row', None, None, 'col')
Inputs may be any that keep to these rules, and one draw needn't show every extreme that they name: tile_map is a permutation of 0 to 15. lower[0, 0, :, 0, :] and lower[1, 0, :, 1, :] are lower triangular with diagonal entries between 2 and 3; lower[0, 0, :, 1, :] is zero.
All inputs are finite; a program needn't handle non-finite values.
Results may differ from a plain program's by a relative error of at most 0.0032.
Values may be sent and summed in bfloat16 or wider, within the bound.
A program may use at most 64 MiB of HBM per device.

v0:
```python
import jax
import jax.numpy as jnp
from jax import lax
from jax.sharding import Mesh
from jax.sharding import PartitionSpec as P

ROW = ("row_0", "row_1")


def spread(shard, axes, root):
    shard = jnp.where(lax.axis_index(axes) == root, shard, jnp.zeros_like(shard))
    for axis in axes:
        shard = lax.psum(shard, axis)
    return shard


def reorder(block, tile_map, tile):
    shape = block.shape
    tiles = block.reshape(shape[:-1] + (shape[-1] // tile, tile))
    return jnp.take(tiles, tile_map, axis=3).reshape(shape)


def body(lower, rhs, tile_map):
    tile = lower.shape[2]
    here = lax.axis_index(ROW)
    whole = lax.all_gather(lower, "col", axis=4, tiled=True)
    panels = whole[0]
    rows = panels.shape[0] * tile
    rhs = lax.all_to_all(
        reorder(
            lax.all_to_all(rhs, "col", split_axis=2, concat_axis=3, tiled=True), tile_map, tile
        ),
        "col",
        split_axis=3,
        concat_axis=2,
        tiled=True,
    )
    work = rhs[0].astype(jnp.float32)
    identity = jnp.eye(tile, dtype=jnp.float32)
    solved_rows = []
    for panel in range(2):
        mine = jnp.where(
            here == panel, jnp.tril(panels[0, :, panel, :].astype(jnp.float32)), identity
        )
        local = jax.scipy.linalg.solve_triangular(mine, work[0], lower=True).astype(jnp.bfloat16)
        solved = spread(local, ROW, panel)
        flat = panels[:, :, panel, :].reshape(rows, tile)
        work = work - jnp.dot(flat, solved, preferred_element_type=jnp.float32).reshape(work.shape)
        solved_rows.append(solved)
    first, second = (solved_rows[0], solved_rows[1])
    result = work.astype(jnp.bfloat16)
    leading = jnp.where(here == 0, first, jnp.where(here == 1, second, result[0]))
    result = result.at[0].set(leading)[None]
    return result


def solution(mesh):
    torus = Mesh(mesh.devices.reshape(8, 4, mesh.shape["col"]), ("row_0", "row_1", "col"))
    return jax.shard_map(
        body,
        mesh=torus,
        in_specs=(P(ROW, None, None, None, "col"), P(ROW, None, None, "col"), P()),
        out_specs=P(ROW, None, None, "col"),
        check_vma=False,
    )
```

profile of v0, /device:TPU:8, one launch (start us, length us, event | category | flops | bytes accessed | tf_op | source)
XLA Modules:
  0.0 522.2 jit_solution(17489380718761430764)
XLA Ops:
  6.5 4.1 copy.38
  10.6 9.4 %all-to-all-start = ((bf16[1,3,512,512]{3,1,0,2:T(4,128)(2,1)}), bf16[1,3,512,512]{3,1,0,2:T(4,128)(2,1)S(1)}, u32[]{:S(2)}, u32[]{:S(2)}) async-start(bf16[1,3,512,512]{3,1,0,2:T(4,128)(2,1)} %copy.38), calls=%async_computation | async-start | bytes 4194304 | tf_op jit(solution)/shard_map/all_to_all | solution.py:31
  20.1 0.9 copy.44
  21.2 56.9 %all-to-all-done = bf16[1,3,512,512]{3,1,0,2:T(4,128)(2,1)S(1)} async-done(((bf16[1,3,512,512]{3,1,0,2:T(4,128)(2,1)}), bf16[1,3,512,512]{3,1,0,2:T(4,128)(2,1)S(1)}, u32[]{:S(2)}, u32[]{:S(2)}) %all-to-all-start) | async-done | bytes 1572896 | tf_op jit(solution)/shard_map/all_to_all | solution.py:31
  78.1 1.5 copy.39
  79.6 2.1 gather_fusion
  81.6 0.9 copy.40
  82.5 0.8 gather.9
  83.5 8.3 %copy.41 = bf16[1,3,32,8192]{2,1,0,3:T(4,128)(2,1)} copy(bf16[1,3,32,8192]{3,2,1,0:T(8,128)(2,1)S(1)} %broadcast_select_fusion) | data formatting | bytes 3145728 | tf_op jit(solution)/shard_map/jit(_take)/select_n | solution.py:20
  91.8 13.2 %reshape.163 = bf16[16,2,24576]{2,1,0:T(2,128)(2,1)} reshape(bf16[8192,1,3,32]{3,2,1,0:T(4,128)(2,1)} %bitcast.122) | data formatting | bytes 3145728
  105.0 8.1 %all-to-all-start.1 = ((bf16[16,2,24576]{2,1,0:T(2,128)(2,1)}), bf16[16,2,24576]{2,1,0:T(2,128)(2,1)}, u32[]{:S(2)}, u32[]{:S(2)}) async-start(bf16[16,2,24576]{2,1,0:T(2,128)(2,1)} %reshape.163), calls=%async_computation.1 | async-start | bytes 3145728 | tf_op jit(solution)/shard_map/all_to_all | solution.py:29
  113.4 7.0 %copy.45 = bf16[1,3,512,2,512]{4,2,3,1,0:T(8,128)(2,1)S(1)} copy(bf16[1,3,512,2,512]{2,3,1,0,4:T(2,128)(2,1)} %all-gather.2.cloned.1.call-done) | data formatting | bytes 6291456 | tf_op jit(solution)/shard_map/all_gather | solution.py:26
  120.5 1.8 fusion.3
  122.7 11.5 %while.5 = (s32[]{:T(128)}, f32[512,512]{1,0:T(8,128)}, s32[4,2]{0,1:T(2,128)S(1)}, f32[4,128,128]{2,1,0:T(8,128)S(1)}, s32[]{:T(128)}) while((s32[]{:T(128)}, f32[512,512]{1,0:T(8,128)}, s32[4,2]{0,1:T(2,128)S(1)}, f32[4,128,128]{2,1,0:T(8,128)S(1)}, s32[]{:T(128)}) %tuple.41), condition=%wide.while_cond.1, body=%wide.while_body.1.sunk | while | flops 2 | bytes 131189 | solution.py:45
  123.4 2.3 bitcast_dynamic-update-slice_fusion.4
  126.3 2.3 bitcast_dynamic-update-slice_fusion.4
  129.2 2.3 bitcast_dynamic-update-slice_fusion.4
  132.1 2.2 bitcast_dynamic-update-slice_fusion.4
  134.3 39.3 %custom-call.4 = f32[4,128,128]{1,2,0:T(8,128)S(1)} custom-call(f32[4,128,128]{2,1,0:T(8,128)S(1)} %get-tuple-element.32), custom_call_target="InvertDiagBlocksLowerTriangular" | custom-call | tf_op jit(solution)/shard_map/jit(_solve_triangular)/triangular_solve | solution.py:45
  173.6 12.6 %reshape.164 = bf16[8192,1,3,32]{3,2,1,0:T(4,128)(2,1)} reshape(bf16[16,2,24576]{2,1,0:T(2,128)(2,1)} %all-to-all-done.1) | data formatting | bytes 3145728
  186.2 9.7 %copy.42 = bf16[1,3,32,8192]{3,2,1,0:T(8,128)(2,1)S(1)} copy(bf16[1,3,32,8192]{2,1,0,3:T(4,128)(2,1)} %bitcast.123) | data formatting | bytes 3145728 | tf_op jit(solution)/shard_map/all_to_all | solution.py:29
  197.2 0.9 copy-done.1
  198.5 1.2 convolution_subtract_fusion.3
  200.2 1.3 convolution_subtract_fusion.2
  202.0 1.6 convolution_subtract_fusion.5
  203.9 0.9 fusion.16
  204.9 83.1 %all-reduce.5.cloned.1.call-done = bf16[512,512]{1,0:T(8,128)(2,1)} async-done(((bf16[512,512]{1,0:T(8,128)(2,1)}), bf16[512,512]{1,0:T(8,128)(2,1)}) %all-reduce.5.cloned.1.call-update) | async-done | bytes 524304 | tf_op jit(solution)/shard_map/psum | solution.py:13
  289.0 13.6 %while.6 = (s32[]{:T(128)}, f32[512,512]{1,0:T(8,128)}, s32[4,2]{0,1:T(2,128)S(1)}, f32[4,128,128]{2,1,0:T(8,128)}, s32[]{:T(128)}) while((s32[]{:T(128)}, f32[512,512]{1,0:T(8,128)}, s32[4,2]{0,1:T(2,128)S(1)}, f32[4,128,128]{2,1,0:T(8,128)}, s32[]{:T(128)}) %tuple.57), condition=%wide.while_cond.1.clone, body=%wide.while_body.1.clone.sunk | while | flops 2 | bytes 132205 | solution.py:45
  289.6 2.8 bitcast_dynamic-update-slice_fusion.5
  293.0 2.8 bitcast_dynamic-update-slice_fusion.5
  296.4 2.8 bitcast_dynamic-update-slice_fusion.5
  299.8 2.7 bitcast_dynamic-update-slice_fusion.5
  302.6 3.7 copy.43
  306.3 40.1 %custom-call.5 = f32[4,128,128]{1,2,0:T(8,128)S(1)} custom-call(f32[4,128,128]{2,1,0:T(8,128)} %get-tuple-element.33), custom_call_target="InvertDiagBlocksLowerTriangular" | custom-call | tf_op jit(solution)/shard_map/jit(_solve_triangular)/triangular_solve | solution.py:45
  346.4 4.0 fusion.50
  350.4 4.3 convolution_bitcast_fusion.1
  354.7 3.6 copy.47
  358.2 2.6 sub.25
  361.4 1.3 convolution_subtract_fusion.1
  363.1 1.3 convolution_subtract_fusion
  364.9 1.6 convolution_subtract_fusion.4
  366.9 0.9 fusion.15
  368.1 77.8 %all-reduce.9.cloned.1.call-done = bf16[512,512]{1,0:T(8,128)(2,1)} async-done(((bf16[512,512]{1,0:T(8,128)(2,1)}), bf16[512,512]{1,0:T(8,128)(2,1)}) %all-reduce.9.cloned.1.call-update) | async-done | bytes 524304 | tf_op jit(solution)/shard_map/psum | solution.py:13
  445.9 54.0 %all-reduce.11.cloned.1.call-done = bf16[512,512]{1,0:T(8,128)(2,1)} async-done(((bf16[512,512]{1,0:T(8,128)(2,1)}), bf16[512,512]{1,0:T(8,128)(2,1)}) %all-reduce.11.cloned.1.call-update) | async-done | bytes 524304 | tf_op jit(solution)/shard_map/psum | solution.py:13
  499.9 4.3 convolution_bitcast_fusion
  504.2 3.6 copy.50
  507.8 5.2 fusion.1
  513.0 2.7 fusion.21
  (64 shorter events, 12.0 us)
Async XLA Ops:
  10.6 9.5 %copy-start.5 = (bf16[1,3,512,2,32]{2,4,3,1,0:T(8,128)(2,1)S(1)}, bf16[1,3,512,2,32]{2,4,3,1,0:T(8,128)(2,1)}, u32[]{:S(2)}) copy-start(bf16[1,3,512,2,32]{2,4,3,1,0:T(8,128)(2,1)} %param.7) | copy-start | bytes 589828
  10.6 10.4 %copy-start.6 = (s32[16]{0:T(128)S(1)}, s32[16]{0:T(128)}, u32[]{:S(2)}) copy-start(s32[16]{0:T(128)} %param.9) | copy-start | bytes 196
  10.6 67.4 %all-to-all-start = ((bf16[1,3,512,512]{3,1,0,2:T(4,128)(2,1)}), bf16[1,3,512,512]{3,1,0,2:T(4,128)(2,1)S(1)}, u32[]{:S(2)}, u32[]{:S(2)}) async-start(bf16[1,3,512,512]{3,1,0,2:T(4,128)(2,1)} %copy.38), calls=%async_computation | async-start | bytes 4194304 | tf_op jit(solution)/shard_map/all_to_all | solution.py:31
  20.1 93.4 %all-gather.2.cloned.1.call-start = ((), (), s32[]{:S(2)}) async-start(), calls=%async_computation.2 | async-start | bytes 3342336 | tf_op jit(solution)/shard_map/all_gather | solution.py:26
  105.0 68.5 %all-to-all-start.1 = ((bf16[16,2,24576]{2,1,0:T(2,128)(2,1)}), bf16[16,2,24576]{2,1,0:T(2,128)(2,1)}, u32[]{:S(2)}, u32[]{:S(2)}) async-start(bf16[16,2,24576]{2,1,0:T(2,128)(2,1)} %reshape.163), calls=%async_computation.1 | async-start | bytes 3145728 | tf_op jit(solution)/shard_map/all_to_all | solution.py:29
  113.2 174.8 %all-reduce.5.cloned.1.call-start = ((), (), s32[]{:S(2)}) async-start(), calls=%async_computation.3 | async-start | bytes 1048576 | tf_op jit(solution)/shard_map/psum | solution.py:13
  120.5 2.2 copy-start
  196.5 1.7 copy-start.1
  204.9 145.5 %all-reduce.7.cloned.1.call-start = ((), (), s32[]{:S(2)}) async-start(), calls=%async_computation.4 | async-start | bytes 1048576 | tf_op jit(solution)/shard_map/psum | solution.py:13
  288.0 157.9 %all-reduce.9.cloned.1.call-start = ((), (), s32[]{:S(2)}) async-start(), calls=%async_computation.5 | async-start | bytes 1048576 | tf_op jit(solution)/shard_map/psum | solution.py:13
  360.9 1.8 copy-start.2
  367.8 132.1 %all-reduce.11.cloned.1.call-start = ((), (), s32[]{:S(2)}) async-start(), calls=%async_computation.6 | async-start | bytes 1048576 | tf_op jit(solution)/shard_map/psum | solution.py:13
  507.8 5.2 copy-start.3
  507.8 5.2 copy-start.4
Sparse Core Ops, SparseCore 0:
  23.0 65.0 all-gather.1
  205.0 82.9 all-reduce.4
  290.4 51.8 all-reduce.6
  367.9 77.9 all-reduce.8
  448.1 51.7 all-reduce.10
where the time goes:
time: 524 us; the launch traced here: 522 us
  waiting for transfers between devices  272 us (52%)
  local copies, waits for them, and re-layouts  104 us (20%)
  other arithmetic  93.7 us (18%)
  matrix products  20.2 us (4%)
  starting transfers between devices  18.4 us (4%)
  between operations  13.5 us (3%)
    psum x4, waiting for transfers between devices, spread(): shard = lax.psum(shard, axis)  215 us
    another operation x4, other arithmetic, body(): jax.scipy.linalg.solve_triangular(mine, work[0], lower=True)  81.2 us
    all_to_all x1, waiting for transfers between devices, body(): lax.all_to_all(rhs, 'col', split_axis=2, concat_axis=3, tiled=True)  56.9 us
    unnamed x21, local copies, waits for them, and re-layouts  32.9 us
    another operation x27, local copies, waits for them, and re-layouts, body(): jax.scipy.linalg.solve_triangular(mine, work[0], lower=True)  25.7 us
    another operation x14, matrix products, body(): jax.scipy.linalg.solve_triangular(mine, work[0], lower=True)  11.6 us
  transfers between devices with their start and end apart: 7, of which 4 were waited for; matrix products, arithmetic and copies ran while one was open for 29% of the time, Pallas kernels for 0%

commit v1 on v0

--- a/solution.py
+++ b/solution.py
@@ -7,10 +7,16 @@
 ROW = ("row_0", "row_1")
 
 
+def add_all(x, name):
+    parts = lax.all_gather(x, name, axis=0, tiled=False)
+    total = parts.sum(axis=0)
+    return total
+
+
 def spread(shard, axes, root):
     shard = jnp.where(lax.axis_index(axes) == root, shard, jnp.zeros_like(shard))
     for axis in axes:
-        shard = lax.psum(shard, axis)
+        shard = add_all(shard, axis)
     return shard
 
 

time: 524 us -> 473 us (0.903)
  the two profiles are of different devices: /device:TPU:8 before, /device:TPU:1 now
where the time goes in v1:
time: 473 us; the launch traced here: 471 us
  waiting for transfers between devices  210 us (44%)
  other arithmetic  107 us (23%)
  local copies, waits for them, and re-layouts  102 us (22%)
  matrix products  20.3 us (4%)
  starting transfers between devices  17.6 us (4%)
  between operations  13.5 us (3%)
    all_gather x4, waiting for transfers between devices, add_all(): parts = lax.all_gather(x, name, axis=0, tiled=False)  151 us
    another operation x4, other arithmetic, body(): jax.scipy.linalg.solve_triangular(mine, work[0], lower=True)  81.2 us
    all_to_all x1, waiting for transfers between devices, body(): lax.all_to_all(rhs, 'col', split_axis=2, concat_axis=3, tiled=True)  58.8 us
    unnamed x23, local copies, waits for them, and re-layouts  33.6 us
    another operation x27, local copies, waits for them, and re-layouts, body(): jax.scipy.linalg.solve_triangular(mine, work[0], lower=True)  22.8 us
    reduce_sum x4, other arithmetic, add_all(): total = parts.sum(axis=0)  13.2 us
    another operation x14, matrix products, body(): jax.scipy.linalg.solve_triangular(mine, work[0], lower=True)  11.6 us
    all_to_all x1, starting transfers between devices, body(): lax.all_to_all(rhs, 'col', split_axis=2, concat_axis=3, tiled=True)  10.5 us
  transfers between devices with their start and end apart: 7, of which 4 were waited for; matrix products, arithmetic and copies ran while one was open for 31% of the time, Pallas kernels for 0%

profile of v1, /device:TPU:1, one launch (start us, length us, event | category | flops | bytes accessed | tf_op | source)
XLA Modules:
  0.0 470.9 jit_solution(5780092272472809311)
XLA Ops:
  6.5 4.1 copy.51
  10.6 10.5 %all-to-all-start = ((bf16[1,3,512,512]{3,1,0,2:T(4,128)(2,1)}), bf16[1,3,512,512]{3,1,0,2:T(4,128)(2,1)S(1)}, u32[]{:S(2)}, u32[]{:S(2)}) async-start(bf16[1,3,512,512]{3,1,0,2:T(4,128)(2,1)} %copy.51), calls=%async_computation | async-start | bytes 4194304 | tf_op jit(solution)/shard_map/all_to_all | solution.py:37
  22.2 58.8 %all-to-all-done = bf16[1,3,512,512]{3,1,0,2:T(4,128)(2,1)S(1)} async-done(((bf16[1,3,512,512]{3,1,0,2:T(4,128)(2,1)}), bf16[1,3,512,512]{3,1,0,2:T(4,128)(2,1)S(1)}, u32[]{:S(2)}, u32[]{:S(2)}) %all-to-all-start) | async-done | bytes 1572896 | tf_op jit(solution)/shard_map/all_to_all | solution.py:37
  81.0 1.5 copy.52
  82.5 2.1 gather_fusion
  86.4 8.3 %copy.54 = bf16[1,3,32,8192]{2,1,0,3:T(4,128)(2,1)} copy(bf16[1,3,32,8192]{3,2,1,0:T(8,128)(2,1)S(1)} %broadcast_select_fusion) | data formatting | bytes 3145728 | tf_op jit(solution)/shard_map/jit(_take)/select_n | solution.py:26
  94.7 13.2 %reshape.182 = bf16[16,2,24576]{2,1,0:T(2,128)(2,1)} reshape(bf16[8192,1,3,32]{3,2,1,0:T(4,128)(2,1)} %bitcast.124) | data formatting | bytes 3145728
  107.9 6.2 %all-to-all-start.1 = ((bf16[16,2,24576]{2,1,0:T(2,128)(2,1)}), bf16[16,2,24576]{2,1,0:T(2,128)(2,1)}, u32[]{:S(2)}, u32[]{:S(2)}) async-start(bf16[16,2,24576]{2,1,0:T(2,128)(2,1)} %reshape.182), calls=%async_computation.1 | async-start | bytes 3145728 | tf_op jit(solution)/shard_map/all_to_all | solution.py:35
  114.5 7.0 %copy.58 = bf16[1,3,512,2,512]{4,2,3,1,0:T(8,128)(2,1)S(1)} copy(bf16[1,3,512,2,512]{2,3,1,0,4:T(2,128)(2,1)} %all-gather.10.cloned.1.call-done) | data formatting | bytes 6291456 | tf_op jit(solution)/shard_map/all_gather | solution.py:32
  121.5 1.8 fusion.3
  123.7 11.6 %while.5 = (s32[]{:T(128)}, f32[512,512]{1,0:T(8,128)}, s32[4,2]{0,1:T(2,128)S(1)}, f32[4,128,128]{2,1,0:T(8,128)S(1)}, s32[]{:T(128)}) while((s32[]{:T(128)}, f32[512,512]{1,0:T(8,128)}, s32[4,2]{0,1:T(2,128)S(1)}, f32[4,128,128]{2,1,0:T(8,128)S(1)}, s32[]{:T(128)}) %tuple.41), condition=%wide.while_cond.1, body=%wide.while_body.1.sunk | while | flops 2 | bytes 131189 | solution.py:51
  124.4 2.3 bitcast_dynamic-update-slice_fusion.4
  127.3 2.3 bitcast_dynamic-update-slice_fusion.4
  130.3 2.3 bitcast_dynamic-update-slice_fusion.4
  133.2 2.2 bitcast_dynamic-update-slice_fusion.4
  135.4 39.3 %custom-call.4 = f32[4,128,128]{1,2,0:T(8,128)S(1)} custom-call(f32[4,128,128]{2,1,0:T(8,128)S(1)} %get-tuple-element.32), custom_call_target="InvertDiagBlocksLowerTriangular" | custom-call | tf_op jit(solution)/shard_map/jit(_solve_triangular)/triangular_solve | solution.py:51
  174.7 12.6 %reshape.183 = bf16[8192,1,3,32]{3,2,1,0:T(4,128)(2,1)} reshape(bf16[16,2,24576]{2,1,0:T(2,128)(2,1)} %all-to-all-done.1) | data formatting | bytes 3145728
  187.3 9.7 %copy.55 = bf16[1,3,32,8192]{3,2,1,0:T(8,128)(2,1)S(1)} copy(bf16[1,3,32,8192]{2,1,0,3:T(4,128)(2,1)} %bitcast.125) | data formatting | bytes 3145728 | tf_op jit(solution)/shard_map/all_to_all | solution.py:35
  198.3 1.0 copy-done.1
  199.7 1.2 convolution_subtract_fusion.3
  201.3 1.3 convolution_subtract_fusion.2
  203.1 1.6 convolution_subtract_fusion.5
  206.1 61.0 %all-gather.12.cloned.1.call-done = bf16[4096,512]{1,0:T(8,128)(2,1)} async-done(((bf16[512,512]{1,0:T(8,128)(2,1)}), bf16[4096,512]{1,0:T(8,128)(2,1)}) %all-gather.12.cloned.1.call-update) | async-done | bytes 4194320 | tf_op jit(solution)/shard_map/all_gather | solution.py:11
  267.1 3.7 reduce_sum.52
  271.1 3.7 copy.56
  274.9 11.3 %while.6 = (s32[]{:T(128)}, f32[512,512]{1,0:T(8,128)}, s32[4,2]{0,1:T(2,128)S(1)}, f32[4,128,128]{2,1,0:T(8,128)S(1)}, s32[]{:T(128)}) while((s32[]{:T(128)}, f32[512,512]{1,0:T(8,128)}, s32[4,2]{0,1:T(2,128)S(1)}, f32[4,128,128]{2,1,0:T(8,128)S(1)}, s32[]{:T(128)}) %tuple.57), condition=%wide.while_cond.1.clone, body=%wide.while_body.1.clone.sunk | while | flops 2 | bytes 131189 | solution.py:51
  275.5 2.2 bitcast_dynamic-update-slice_fusion.5
  278.3 2.2 bitcast_dynamic-update-slice_fusion.5
  281.1 2.2 bitcast_dynamic-update-slice_fusion.5
  284.0 2.2 bitcast_dynamic-update-slice_fusion.5
  286.9 40.1 %custom-call.5 = f32[4,128,128]{1,2,0:T(8,128)S(1)} custom-call(f32[4,128,128]{2,1,0:T(8,128)} %copy-done.5), custom_call_target="InvertDiagBlocksLowerTriangular" | custom-call | tf_op jit(solution)/shard_map/jit(_solve_triangular)/triangular_solve | solution.py:51
  327.0 4.0 fusion.49
  330.9 2.9 reduce_sum.53
  333.8 4.3 convolution_bitcast_fusion.1
  338.1 3.6 copy.60
  341.7 2.6 sub.25
  344.9 1.3 convolution_subtract_fusion.1
  346.6 1.3 convolution_subtract_fusion
  348.4 1.6 convolution_subtract_fusion.4
  350.4 0.9 fusion.15
  351.6 56.1 %all-gather.16.cloned.1.call-done = bf16[4096,512]{1,0:T(8,128)(2,1)} async-done(((bf16[512,512]{1,0:T(8,128)(2,1)}), bf16[4096,512]{1,0:T(8,128)(2,1)}) %all-gather.16.cloned.1.call-update) | async-done | bytes 4194320 | tf_op jit(solution)/shard_map/all_gather | solution.py:11
  407.7 3.7 reduce_sum.54
  411.4 34.3 %all-gather.18.cloned.1.call-done = bf16[2048,512]{1,0:T(8,128)(2,1)} async-done(((bf16[512,512]{1,0:T(8,128)(2,1)}), bf16[2048,512]{1,0:T(8,128)(2,1)}) %all-gather.18.cloned.1.call-update) | async-done | bytes 2097168 | tf_op jit(solution)/shard_map/all_gather | solution.py:11
  445.8 2.9 reduce_sum.55
  448.6 4.4 convolution_bitcast_fusion
  453.0 3.5 copy.63
  456.5 5.2 %fusion.1 = bf16[1,3,512,512]{3,2,1,0:T(8,128)(2,1)} fusion(f32[1,3,512,512]{3,2,1,0:T(8,128)} %bitcast.133, f32[1,3,512,512]{3,2,1,0:T(8,128)} %bitcast.128, f32[1,3,16,32,512]{4,3,2,1,0:T(8,128)S(1)} %copy.56), kind=kLoop, calls=%fused_computation.9 | loop fusion | flops 2359296 | bytes 11010048 | tf_op jit(solution)/shard_map/convert_element_type | solution.py:57
  461.7 2.7 fusion.20
  (70 shorter events, 15.6 us)
Async XLA Ops:
  10.6 10.5 %copy-start.6 = (bf16[1,3,512,2,32]{2,4,3,1,0:T(8,128)(2,1)S(1)}, bf16[1,3,512,2,32]{2,4,3,1,0:T(8,128)(2,1)}, u32[]{:S(2)}) copy-start(bf16[1,3,512,2,32]{2,4,3,1,0:T(8,128)(2,1)} %param.7) | copy-start | bytes 589828
  10.6 11.4 %copy-start.7 = (s32[16]{0:T(128)S(1)}, s32[16]{0:T(128)}, u32[]{:S(2)}) copy-start(s32[16]{0:T(128)} %param.9) | copy-start | bytes 196
  10.6 70.3 %all-to-all-start = ((bf16[1,3,512,512]{3,1,0,2:T(4,128)(2,1)}), bf16[1,3,512,512]{3,1,0,2:T(4,128)(2,1)S(1)}, u32[]{:S(2)}, u32[]{:S(2)}) async-start(bf16[1,3,512,512]{3,1,0,2:T(4,128)(2,1)} %copy.51), calls=%async_computation | async-start | bytes 4194304 | tf_op jit(solution)/shard_map/all_to_all | solution.py:37
  21.1 93.4 %all-gather.10.cloned.1.call-start = ((), (), s32[]{:S(2)}) async-start(), calls=%async_computation.2 | async-start | bytes 3342336 | tf_op jit(solution)/shard_map/all_gather | solution.py:32
  107.9 66.8 %all-to-all-start.1 = ((bf16[16,2,24576]{2,1,0:T(2,128)(2,1)}), bf16[16,2,24576]{2,1,0:T(2,128)(2,1)}, u32[]{:S(2)}, u32[]{:S(2)}) async-start(bf16[16,2,24576]{2,1,0:T(2,128)(2,1)} %reshape.182), calls=%async_computation.1 | async-start | bytes 3145728 | tf_op jit(solution)/shard_map/all_to_all | solution.py:35
  114.2 152.9 %all-gather.12.cloned.1.call-start = ((), (), s32[]{:S(2)}) async-start(), calls=%async_computation.3 | async-start | bytes 4718592 | tf_op jit(solution)/shard_map/all_gather | solution.py:11
  121.5 2.2 copy-start
  197.6 1.7 copy-start.1
  206.0 124.9 %all-gather.14.cloned.1.call-start = ((), (), s32[]{:S(2)}) async-start(), calls=%async_computation.4 | async-start | bytes 2621440 | tf_op jit(solution)/shard_map/all_gather | solution.py:11
  270.9 136.8 %all-gather.16.cloned.1.call-start = ((), (), s32[]{:S(2)}) async-start(), calls=%async_computation.5 | async-start | bytes 4718592 | tf_op jit(solution)/shard_map/all_gather | solution.py:11
  286.2 0.7 copy-start.5
  344.3 1.8 copy-start.2
  351.3 94.5 %all-gather.18.cloned.1.call-start = ((), (), s32[]{:S(2)}) async-start(), calls=%async_computation.6 | async-start | bytes 2621440 | tf_op jit(solution)/shard_map/all_gather | solution.py:11
  456.5 5.2 %copy-start.3 = (bf16[512,512]{1,0:T(8,128)(2,1)S(1)}, bf16[512,512]{1,0:T(8,128)(2,1)}, u32[]{:S(2)}) copy-start(bf16[512,512]{1,0:T(8,128)(2,1)} %reduce_sum.53) | copy-start | bytes 1572868
  456.5 5.2 %copy-start.4 = (bf16[512,512]{1,0:T(8,128)(2,1)S(1)}, bf16[512,512]{1,0:T(8,128)(2,1)}, u32[]{:S(2)}) copy-start(bf16[512,512]{1,0:T(8,128)(2,1)} %reduce_sum.55) | copy-start | bytes 1572868
Sparse Core Ops, SparseCore 0:
  24.0 65.5 all-gather.9
  206.1 60.9 all-gather.11
  271.0 34.1 all-gather.13
  351.4 56.2 all-gather.15
  411.6 34.1 all-gather.17
